TPU v7x, 256 devices: a whole 4x4x8 slice. The times are simulated.
256 devices in a mesh: group: 64 (over z, y_hi, x), replica: 4 (over y_lo, core).
Axes of the slice: x: 4, y: 4 (y_hi: 2, y_lo: 2; y = y_hi * 2 + y_lo), z: 8, core: 2. Of those that a mesh axis runs over, the one named last changes fastest.
Arguments:
- grad: bfloat16 [32768, 8192], P('group', 'replica'), may hold values from -45 to 45, as said below
- prev_left: bfloat16 [64, 512, 512], P('group', 'replica'), may hold values from -1 to 1.5
- prev_right: bfloat16 [16, 512, 512], P('replica', 'group'), may hold values from -1 to 1.5
- exp_left: int32 [64], P('group'), may hold values from -2 to 2
- exp_right: int32 [16], P('replica'), may hold values from -2 to 2
- strip_owner: int32 [64], replicated, may hold values from 0 to 63, each once
Outputs:
- precond: bfloat16 [32768, 8192], P('group', 'replica')
- root_left: bfloat16 [64, 512, 512], P('group', 'replica')
- root_right: bfloat16 [16, 64, 8, 512], P('replica', 'group')
Inputs may be any that keep to these rules, and one draw needn't show every extreme that they name: `grad`: entries have row and column scales of different sizes. `strip_owner`: each of 0 to 63 appears once.
All inputs are finite; a program needn't handle non-finite values.
Results may differ from a plain program's by a relative error of at most 0.0083.
Values may be sent and summed in bfloat16 or wider, within the bound.
A program may use at most 64 MiB of HBM per device.

v0:
```python
import jax
import jax.numpy as jnp
from jax import lax
from jax.sharding import Mesh
from jax.sharding import PartitionSpec as P

GROUP = ("group_0", "group_1", "group_2")
REPLICA = ("replica_0", "replica_1")
GROUP_REPLICA = ("group_0", "group_1", "group_2", "replica_0", "replica_1")
EPSILON = 1e-06


def over_axes(x, axes):
    for axis in axes:
        x = lax.psum(x, axis)
    return x


def cut_along(x, dim, devices):
    dims = x.shape
    pieces = x.reshape(*dims[:dim], devices, dims[dim] // devices, *dims[dim + 1 :])
    return jnp.moveaxis(pieces, dim, 0)


def sent_and_summed(x, axis, dim):
    pieces = cut_along(x, dim, lax.axis_size(axis))
    arrived = lax.all_to_all(pieces, axis, split_axis=0, concat_axis=0, tiled=True)
    return arrived.astype(jnp.float32).sum(axis=0)


def from_everyone(x, axis):
    copies = jnp.broadcast_to(x, (lax.axis_size(axis), *x.shape))
    return lax.all_to_all(copies, axis, split_axis=0, concat_axis=0, tiled=True)


def in_order(pieces, dim):
    pieces = jnp.moveaxis(pieces, 0, dim)
    dims = pieces.shape
    return pieces.reshape(*dims[:dim], dims[dim] * dims[dim + 1], *dims[dim + 2 :])


def collect(x, axis, dim):
    pieces = from_everyone(x, axis)
    return in_order(pieces, dim)


def pow_two(exponent):
    result = jnp.zeros(exponent.shape, jnp.float32)
    for power in range(-4, 5):
        result = result + jnp.where(exponent == power, jnp.float32(2.0**power), jnp.float32(0.0))
    return result


def newton_rows(gram_rows, gram_scale, start_root, start_rows):
    product = gram_rows / gram_scale
    for repeat in range(5):
        product = jnp.matmul(product, start_root, precision=lax.Precision.HIGHEST)
    return (5.0 * start_rows - product) / 4.0


def shards(grad, prev_left, prev_right, exp_left, exp_right, strip_owner):
    block_size = grad.shape[0]
    col_count = prev_right.shape[0]
    pieces = grad.reshape(block_size, col_count, block_size)
    groups = lax.axis_size(GROUP)
    replicas = lax.axis_size(REPLICA)
    group_index = lax.axis_index(GROUP)
    replica_index = lax.axis_index(REPLICA)
    strip_rows = block_size // groups
    square = jnp.sum(jnp.square(pieces.astype(jnp.float32)), axis=(0, 2))
    group_pick = (jnp.arange(groups) == group_index).astype(jnp.float32)
    replica_pick = (jnp.arange(replicas) == replica_index).astype(jnp.float32)
    norm_grid = group_pick[:, None, None] * replica_pick[None, :, None] * square[None, None, :]
    norm_grid = over_axes(norm_grid, GROUP_REPLICA)
    left_scale = jnp.sum(norm_grid * group_pick[:, None, None]) / block_size + EPSILON
    right_scale = (
        jnp.sum(norm_grid * replica_pick[None, :, None], axis=(0, 1)) / block_size + EPSILON
    )
    left_part = lax.dot_general(
        grad, grad, (((1,), (1,)), ((), ())), preferred_element_type=jnp.float32
    )
    right_part = lax.dot_general(
        pieces, pieces, (((0,), (0,)), ((1,), (1,))), preferred_element_type=jnp.float32
    )
    left_strip = sent_and_summed(left_part.astype(jnp.bfloat16), REPLICA, 0)
    owned_strip = strip_owner[group_index]
    reordered = right_part.reshape(col_count, groups, strip_rows, block_size)[:, strip_owner]
    reordered = reordered.reshape(col_count, block_size, block_size)
    right_strip = sent_and_summed(reordered.astype(jnp.bfloat16), GROUP, 1)
    left_start = collect(prev_left[0], REPLICA, 0).astype(jnp.float32)
    right_start = lax.all_gather(prev_right, GROUP, axis=1, tiled=True).astype(jnp.float32)
    left_rows = prev_left[0].astype(jnp.float32)
    right_rows = lax.dynamic_slice_in_dim(right_start, owned_strip * strip_rows, strip_rows, 1)
    left_new = newton_rows(left_strip, left_scale, left_start, left_rows)
    right_new = newton_rows(right_strip, right_scale[:, None, None], right_start, right_rows)
    left_code = (left_new * pow_two(-exp_left[0])).astype(jnp.bfloat16)
    right_code = (right_new * pow_two(-exp_right)[:, None, None]).astype(jnp.bfloat16)
    left_full = collect(left_code, REPLICA, 0)
    right_owned = lax.all_gather(right_code, GROUP, axis=1, tiled=True).reshape(
        col_count, groups, strip_rows, block_size
    )
    owner_match = strip_owner[:, None] == jnp.arange(groups)[None, :]
    inverse = jnp.sum(jnp.where(owner_match, jnp.arange(groups)[:, None], 0), axis=0)
    right_full = right_owned[:, inverse].reshape(col_count, block_size, block_size)
    left_dec = (left_full.astype(jnp.float32) * pow_two(exp_left[0])).astype(jnp.bfloat16)
    right_dec = (right_full.astype(jnp.float32) * pow_two(exp_right)[:, None, None]).astype(
        jnp.bfloat16
    )
    middle = lax.dot_general(
        pieces, right_dec, (((2,), (1,)), ((1,), (0,))), preferred_element_type=jnp.float32
    ).astype(jnp.bfloat16)
    result = lax.dot_general(
        left_dec, middle, (((1,), (1,)), ((), ())), preferred_element_type=jnp.float32
    ).astype(jnp.bfloat16)
    return (
        result.reshape(block_size, col_count * block_size),
        left_code[None],
        right_code[:, None],
    )


def solution(mesh):
    torus = Mesh(
        mesh.devices.reshape(8, 2, 4, 2, 2),
        ("group_0", "group_1", "group_2", "replica_0", "replica_1"),
    )
    in_specs = (
        P(GROUP, REPLICA),
        P(GROUP, REPLICA, None),
        P(REPLICA, GROUP, None),
        P(GROUP),
        P(REPLICA),
        P(),
    )
    out_specs = (P(GROUP, REPLICA), P(GROUP, REPLICA, None), P(REPLICA, GROUP, None, None))
    return jax.shard_map(
        shards, mesh=torus, in_specs=in_specs, out_specs=out_specs, check_vma=False
    )
```

profile of v0, /device:TPU:2, one launch (start us, length us, event | category | flops | bytes accessed | tf_op | source)
XLA Modules:
  0.0 278.3 jit_solution(7575325970475510265)
XLA Ops:
  7.2 3.5 %convolution_bitcast_fusion = bf16[4,64,8,512]{3,2,1,0:T(8,128)(2,1)S(1)} fusion(bf16[64,4,8,512]{3,2,1,0:T(8,128)(2,1)} %bitcast.77), kind=kOutput, calls=%fused_computation.7 | convolution fusion | flops 1073741824 | bytes 4194304 | tf_op jit(solution)/shard_map/dot_general | solution.py:82
  10.8 2.0 gather_fusion
  12.8 14.6 %all-to-all-start.3 = ((bf16[64,4,8,512]{3,2,1,0:T(8,128)(2,1)}), bf16[64,4,8,512]{3,2,1,0:T(8,128)(2,1)S(1)}, u32[]{:S(2)}, u32[]{:S(2)}) async-start(bf16[64,4,8,512]{3,2,1,0:T(8,128)(2,1)} %gather_fusion), calls=%async_computation.3 | async-start | bytes 4194304 | tf_op jit(solution)/shard_map/all_to_all | solution.py:27
  27.5 0.7 all-gather.3.cloned.1.call-update
  28.2 0.6 dynamic_slice.6
  29.5 2.0 multiply_reduce_fusion
  31.8 53.5 %psum.35 = f32[64,4,4]{0,2,1:T(4,128)S(1)} all-reduce(f32[64,4,4]{0,2,1:T(4,128)S(1)} %broadcast_multiply_fusion), channel_id=1, replica_groups=mesh['group_0'=8,'group_1'=2,'group_2'=4,'replica_0'=2,'replica_1'=2] {'..., use_global_device_ids=true, to_apply=%region_3.0 | all-reduce | flops 1024 | bytes 8192 | tf_op jit(solution)/shard_map/psum | solution.py:15
  85.3 6.5 %psum.36 = f32[64,4,4]{0,2,1:T(4,128)S(1)} all-reduce(f32[64,4,4]{0,2,1:T(4,128)S(1)} %psum.35), channel_id=1, replica_groups=mesh['group_0'=8,'group_1'=2,'group_2'=4,'replica_0'=2,'replica_1'=2] {'..., use_global_device_ids=true, to_apply=%region_4.0 | all-reduce | flops 1024 | bytes 8192 | tf_op jit(solution)/shard_map/psum | solution.py:15
  91.8 8.7 %psum.37 = f32[64,4,4]{0,2,1:T(4,128)S(1)} all-reduce(f32[64,4,4]{0,2,1:T(4,128)S(1)} %psum.36), channel_id=1, replica_groups=mesh['group_0'=8,'group_1'=2,'group_2'=4,'replica_0'=2,'replica_1'=2] {'..., use_global_device_ids=true, to_apply=%region_5.0 | all-reduce | flops 1024 | bytes 8192 | tf_op jit(solution)/shard_map/psum | solution.py:15
  100.5 5.0 %psum.38 = f32[64,4,4]{0,2,1:T(4,128)S(1)} all-reduce(f32[64,4,4]{0,2,1:T(4,128)S(1)} %psum.37), channel_id=1, replica_groups=mesh['group_0'=8,'group_1'=2,'group_2'=4,'replica_0'=2,'replica_1'=2] {'..., use_global_device_ids=true, to_apply=%region_6.0 | all-reduce | flops 1024 | bytes 8192 | tf_op jit(solution)/shard_map/psum | solution.py:15
  105.5 2.5 psum.39
  108.0 0.6 multiply_reduce_fusion.1
  109.0 36.6 %all-gather.3.cloned.1.call-done = bf16[4,512,512]{2,1,0:T(8,128)(2,1)} async-done(((bf16[4,8,512]{2,1,0:T(8,128)(2,1)}), bf16[4,512,512]{2,1,0:T(8,128)(2,1)}) %all-gather.3.cloned.1.call-update) | async-done | bytes 2097168 | tf_op jit(solution)/shard_map/all_gather | solution.py:91
  145.6 2.7 fusion.29
  148.3 0.9 fusion.53
  149.2 0.9 fusion.54
  150.1 0.9 fusion.55
  151.1 1.6 fusion.25
  152.7 1.3 convolution_convert_fusion
  153.9 11.3 %all_to_all.20 = bf16[4,128,512]{2,1,0:T(8,128)(2,1)S(1)} all-to-all(bf16[4,128,512]{2,1,0:T(8,128)(2,1)S(1)} %bitcast.81), channel_id=1, replica_groups=mesh['group_0'=8,'group_1'=2,'group_2'=4,'replica_0'=2,'replica_1'=2] {'..., dimensions={0} | all-to-all | bytes 1048576 | tf_op jit(solution)/shard_map/all_to_all | solution.py:27
  165.3 0.8 broadcast_in_dim.97
  166.1 3.5 %all-to-all-start.1 = ((bf16[4,128,512]{2,1,0:T(8,128)(2,1)}), bf16[4,128,512]{2,1,0:T(8,128)(2,1)S(1)}, u32[]{:S(2)}, u32[]{:S(2)}) async-start(bf16[4,128,512]{2,1,0:T(8,128)(2,1)} %broadcast_in_dim.97), calls=%async_computation.1 | async-start | bytes 1048576 | tf_op jit(solution)/shard_map/all_to_all | solution.py:33
  171.1 7.3 %all-to-all-done.1 = bf16[4,128,512]{2,1,0:T(8,128)(2,1)S(1)} async-done(((bf16[4,128,512]{2,1,0:T(8,128)(2,1)}), bf16[4,128,512]{2,1,0:T(8,128)(2,1)S(1)}, u32[]{:S(2)}, u32[]{:S(2)}) %all-to-all-start.1) | async-done | bytes 524320 | tf_op jit(solution)/shard_map/all_to_all | solution.py:33
  179.1 0.4 fusion.51
  179.9 0.4 fusion.23
  180.3 0.8 broadcast_in_dim.98
  181.2 3.7 %all-to-all-start.2 = ((bf16[4,128,512]{2,1,0:T(8,128)(2,1)}), bf16[4,128,512]{2,1,0:T(8,128)(2,1)S(1)}, u32[]{:S(2)}, u32[]{:S(2)}) async-start(bf16[4,128,512]{2,1,0:T(8,128)(2,1)} %broadcast_in_dim.98), calls=%async_computation.2 | async-start | bytes 1048576 | tf_op jit(solution)/shard_map/all_to_all | solution.py:33
  184.9 8.5 %all-to-all-done.2 = bf16[4,128,512]{2,1,0:T(8,128)(2,1)S(1)} async-done(((bf16[4,128,512]{2,1,0:T(8,128)(2,1)}), bf16[4,128,512]{2,1,0:T(8,128)(2,1)S(1)}, u32[]{:S(2)}, u32[]{:S(2)}) %all-to-all-start.2) | async-done | bytes 524320 | tf_op jit(solution)/shard_map/all_to_all | solution.py:33
  193.5 65.0 %all-gather.5.cloned.1.call-done = bf16[4,512,512]{2,1,0:T(8,128)(2,1)} async-done(((bf16[4,8,512]{2,1,0:T(8,128)(2,1)}), bf16[4,512,512]{2,1,0:T(8,128)(2,1)}) %all-gather.5.cloned.1.call-update) | async-done | bytes 2097168 | tf_op jit(solution)/shard_map/all_gather | solution.py:99
  258.5 3.6 %gather_fusion.1 = bf16[64,4,8,512]{3,2,1,0:T(8,128)(2,1)} fusion(bf16[4,64,8,512]{3,2,1,0:T(8,128)(2,1)} %bitcast.79, s32[1024]{0:T(1024)S(1)} %pad_clamp_fusion), kind=kCustom, calls=%fused_computation.1 | custom fusion | bytes 4194560 | tf_op jit(solution)/shard_map/gather | solution.py:104
  262.1 5.5 %fusion.9 = bf16[512,4,512]{0,2,1:T(8,128)(2,1)} fusion(bf16[512,512,1]{1,0,2:T(8,128)(2,1)S(1)} %bitcast.82, f32[4]{0:T(128)S(1)} %get-tuple-element.17, bf16[64,4,8,512]{3,2,1,0:T(8,128)(2,1)S(1)} %bitcast.78, bf16[64,4,8,512]{3,2,1,0:T(8,128)(2,1)} %gather_fusion.1), kind=kOutput, calls=%fused_computation.15 | convolution fusion | flops 2152726528 | bytes 6815760 | tf_op jit(solution)/shard_map/dot_general | solution.py:112
  267.6 3.9 %copy.29 = bf16[512,2048]{1,0:T(8,128)(2,1)} copy(bf16[512,2048]{0,1:T(8,128)(2,1)} %bitcast.80) | data formatting | bytes 4194304
  (35 shorter events, 2.1 us)
Async XLA Ops:
  7.2 3.6 %copy-start.5 = (s32[64]{0:T(128)S(1)}, s32[64]{0:T(128)}, u32[]{:S(2)}) copy-start(s32[64]{0:T(128)} %param.11) | copy-start | bytes 772
  12.8 95.9 %all-to-all-start.3 = ((bf16[64,4,8,512]{3,2,1,0:T(8,128)(2,1)}), bf16[64,4,8,512]{3,2,1,0:T(8,128)(2,1)S(1)}, u32[]{:S(2)}, u32[]{:S(2)}) async-start(bf16[64,4,8,512]{3,2,1,0:T(8,128)(2,1)} %gather_fusion), calls=%async_computation.3 | async-start | bytes 4194304 | tf_op jit(solution)/shard_map/all_to_all | solution.py:27
  27.4 81.2 %copy-start.4 = (s32[4]{0:T(128)S(1)}, s32[4]{0:T(128)}, u32[]{:S(2)}) copy-start(s32[4]{0:T(128)} %param.10) | copy-start | bytes 52
  27.4 118.1 %all-gather.3.cloned.1.call-start = ((), (), s32[]{:S(2)}) async-start(), calls=%async_computation.4 | async-start | bytes 2129920 | tf_op jit(solution)/shard_map/all_gather | solution.py:91
  28.2 230.3 %all-gather.5.cloned.1.call-start = ((), (), s32[]{:S(2)}) async-start(), calls=%async_computation.5 | async-start | bytes 2129920 | tf_op jit(solution)/shard_map/all_gather | solution.py:99
  145.6 2.7 copy-start
  150.1 2.5 copy-start.1
  152.7 12.6 %copy-start.2 = (bf16[1,128,512]{2,1,0:T(8,128)(2,1)S(1)}, bf16[1,128,512]{2,1,0:T(8,128)(2,1)}, u32[]{:S(2)}) copy-start(bf16[1,128,512]{2,1,0:T(8,128)(2,1)} %param.7) | copy-start | bytes 393220
  166.1 12.3 %all-to-all-start.1 = ((bf16[4,128,512]{2,1,0:T(8,128)(2,1)}), bf16[4,128,512]{2,1,0:T(8,128)(2,1)S(1)}, u32[]{:S(2)}, u32[]{:S(2)}) async-start(bf16[4,128,512]{2,1,0:T(8,128)(2,1)} %broadcast_in_dim.97), calls=%async_computation.1 | async-start | bytes 1048576 | tf_op jit(solution)/shard_map/all_to_all | solution.py:33
  180.3 81.8 %copy-start.3 = (bf16[128,512]{1,0:T(8,128)(2,1)}, bf16[128,512]{1,0:T(8,128)(2,1)S(1)}, u32[]{:S(2)}) copy-start(bf16[128,512]{1,0:T(8,128)(2,1)S(1)} %fusion.23) | copy-start | bytes 393220
  181.2 12.3 %all-to-all-start.2 = ((bf16[4,128,512]{2,1,0:T(8,128)(2,1)}), bf16[4,128,512]{2,1,0:T(8,128)(2,1)S(1)}, u32[]{:S(2)}, u32[]{:S(2)}) async-start(bf16[4,128,512]{2,1,0:T(8,128)(2,1)} %broadcast_in_dim.98), calls=%async_computation.2 | async-start | bytes 1048576 | tf_op jit(solution)/shard_map/all_to_all | solution.py:33
Sparse Core Ops, SparseCore 0:
  31.7 113.8 all-gather.2
  152.8 105.6 all-gather.4
where the time goes:
time: 279 us; the launch traced here: 278 us
  waiting for transfers between devices  118 us (42%)
  blocking collectives  87.5 us (31%)
  starting transfers between devices  21.8 us (8%)
  matrix products  19.2 us (7%)
  between operations  16.3 us (6%)
  local copies, waits for them, and re-layouts  11.8 us (4%)
  other arithmetic  3.55 us (1%)
    psum x5, blocking collectives, over_axes(): x = lax.psum(x, axis)  76.2 us
    all_gather x1, waiting for transfers between devices, shards(): lax.all_gather(right_code, GROUP, axis=1, tiled=True)  65 us
    all_gather x1, waiting for transfers between devices, shards(): lax.all_gather(prev_right, GROUP, axis=1, tiled=True).astype(jnp.float32)  36.6 us
    all_to_all x2, waiting for transfers between devices, from_everyone(): return lax.all_to_all(copies, axis, split_axis=0, concat_axis=0, tiled=True)  15.8 us
    all_to_all x1, starting transfers between devices, sent_and_summed(): lax.all_to_all(pieces, axis, split_axis=0, concat_axis=0, tiled=True)  14.6 us
    all_to_all x1, blocking collectives, sent_and_summed(): lax.all_to_all(pieces, axis, split_axis=0, concat_axis=0, tiled=True)  11.3 us
    dot_general x10, matrix products, newton_rows(): product = jnp.matmul(product, start_root, precision=lax.Precision.HIGHEST)  8.9 us
    all_to_all x2, starting transfers between devices, from_everyone(): return lax.all_to_all(copies, axis, split_axis=0, concat_axis=0, tiled=True)  7.12 us
  transfers between devices with their start and end apart: 5, of which 4 were waited for; matrix products, arithmetic and copies ran while one was open for 3% of the time, Pallas kernels for 0%

commit v1 on v0

--- a/solution.py
+++ b/solution.py
@@ -96,9 +96,9 @@
     left_code = (left_new * pow_two(-exp_left[0])).astype(jnp.bfloat16)
     right_code = (right_new * pow_two(-exp_right)[:, None, None]).astype(jnp.bfloat16)
     left_full = collect(left_code, REPLICA, 0)
-    right_owned = lax.all_gather(right_code, GROUP, axis=1, tiled=True).reshape(
-        col_count, groups, strip_rows, block_size
-    )
+    right_owned = jnp.concatenate(
+        lax.all_to_all(jnp.stack([right_code] * lax.axis_size(GROUP)), GROUP, 0, 0), axis=1
+    ).reshape(col_count, groups, strip_rows, block_size)
     owner_match = strip_owner[:, None] == jnp.arange(groups)[None, :]
     inverse = jnp.sum(jnp.where(owner_match, jnp.arange(groups)[:, None], 0), axis=0)
     right_full = right_owned[:, inverse].reshape(col_count, block_size, block_size)

time: 279 us -> 256 us (0.918)
  waiting for transfers between devices: 118 us -> 87.6 us
  blocking collectives: 87.5 us -> 75.3 us
  starting transfers between devices: 21.8 us -> 32.9 us
  local copies, waits for them, and re-layouts: 11.8 us -> 17.6 us
    all_gather x1 -> x0, waiting for transfers between devices: 65 us -> none  [shards(): lax.all_gather(right_code, GROUP, axis=1, tiled=True)]
    all_to_all x0 -> x1, waiting for transfers between devices: none -> 46.7 us  [shards(): lax.all_to_all(jnp.stack([right_code] * lax.axis_size(GROUP)), GROUP, 0, 0)]
    all_to_all x2, waiting for transfers between devices: 15.8 us -> 3.68 us  [from_everyone(): return lax.all_to_all(copies, axis, split_axis=0, concat_axis=0, tiled=True)]
    all_to_all x1 -> x0, blocking collectives: 11.3 us -> none  [sent_and_summed(): lax.all_to_all(pieces, axis, split_axis=0, concat_axis=0, tiled=True)]
    all_to_all x0 -> x1, starting transfers between devices: none -> 7.81 us  [shards(): lax.all_to_all(jnp.stack([right_code] * lax.axis_size(GROUP)), GROUP, 0, 0)]
    all_to_all x1 -> x2, starting transfers between devices: 14.6 us -> 18.1 us  [sent_and_summed(): lax.all_to_all(pieces, axis, split_axis=0, concat_axis=0, tiled=True)]
    dot_general x1, matrix products: 1.28 us -> 4.45 us  [shards(): lax.dot_general(grad, grad, (((1,), (1,)), ((), ())), preferred_element_t...]
  transfers between devices with their start and end apart: 5 -> 6, of which waited for: 4 -> 4; matrix products, arithmetic and copies ran while one was open for 3% -> 10% of each run, Pallas kernels for 0% -> 0%
where the time goes in v1:
time: 256 us; the launch traced here: 255 us
  waiting for transfers between devices  87.6 us (34%)
  blocking collectives  75.3 us (29%)
  starting transfers between devices  32.9 us (13%)
  matrix products  20.8 us (8%)
  local copies, waits for them, and re-layouts  17.6 us (7%)
  between operations  16.3 us (6%)
  other arithmetic  4.21 us (2%)
    psum x5, blocking collectives, over_axes(): x = lax.psum(x, axis)  75.3 us
    all_to_all x1, waiting for transfers between devices, shards(): lax.all_to_all(jnp.stack([right_code] * lax.axis_size(GROUP)), GROUP, 0, 0)  46.7 us
    all_gather x1, waiting for transfers between devices, shards(): lax.all_gather(prev_right, GROUP, axis=1, tiled=True).astype(jnp.float32)  34 us
    all_to_all x2, starting transfers between devices, sent_and_summed(): lax.all_to_all(pieces, axis, split_axis=0, concat_axis=0, tiled=True)  18.1 us
    dot_general x10, matrix products, newton_rows(): product = jnp.matmul(product, start_root, precision=lax.Precision.HIGHEST)  8.3 us
    all_to_all x1, starting transfers between devices, shards(): lax.all_to_all(jnp.stack([right_code] * lax.axis_size(GROUP)), GROUP, 0, 0)  7.81 us
    all_to_all x2, starting transfers between devices, from_everyone(): return lax.all_to_all(copies, axis, split_axis=0, concat_axis=0, tiled=True)  6.94 us
    dot_general x1, matrix products, shards(): lax.dot_general(left_dec, middle, (((1,), (1,)), ((), ())), preferred_ele...  5.44 us
  transfers between devices with their start and end apart: 6, of which 4 were waited for; matrix products, arithmetic and copies ran while one was open for 10% of the time, Pallas kernels for 0%

profile of v1, /device:TPU:2, one launch (start us, length us, event | category | flops | bytes accessed | tf_op | source)
XLA Modules:
  0.0 254.7 jit_solution(10504611951206013926)
XLA Ops:
  7.2 1.7 broadcast_in_dim.97
  8.9 3.5 %all-to-all-start.1 = ((bf16[4,128,512]{2,1,0:T(8,128)(2,1)}), bf16[4,128,512]{2,1,0:T(8,128)(2,1)S(1)}, u32[]{:S(2)}, u32[]{:S(2)}) async-start(bf16[4,128,512]{2,1,0:T(8,128)(2,1)} %broadcast_in_dim.97), calls=%async_computation.1 | async-start | bytes 1048576 | tf_op jit(solution)/shard_map/all_to_all | solution.py:33
  12.4 0.7 compare_select_fusion.1
  13.0 4.5 %convolution_convert_fusion = bf16[512,512]{1,0:T(8,128)(2,1)} fusion(bf16[512,2048]{1,0:T(8,128)(2,1)} %param.6), kind=kOutput, calls=%fused_computation.19 | convolution fusion | flops 1074003968 | bytes 2621440 | tf_op jit(solution)/shard_map/dot_general | solution.py:79
  17.5 3.7 %all-to-all-done.1 = bf16[4,128,512]{2,1,0:T(8,128)(2,1)S(1)} async-done(((bf16[4,128,512]{2,1,0:T(8,128)(2,1)}), bf16[4,128,512]{2,1,0:T(8,128)(2,1)S(1)}, u32[]{:S(2)}, u32[]{:S(2)}) %all-to-all-start.1) | async-done | bytes 524320 | tf_op jit(solution)/shard_map/all_to_all | solution.py:33
  21.2 3.5 %all-to-all-start = ((bf16[4,128,512]{2,1,0:T(8,128)(2,1)}), bf16[4,128,512]{2,1,0:T(8,128)(2,1)S(1)}, u32[]{:S(2)}, u32[]{:S(2)}) async-start(bf16[4,128,512]{2,1,0:T(8,128)(2,1)} %bitcast.83), calls=%async_computation | async-start | bytes 1048576 | tf_op jit(solution)/shard_map/all_to_all | solution.py:27
  24.7 2.6 %convolution_bitcast_fusion = bf16[4,64,8,512]{3,2,1,0:T(8,128)(2,1)} fusion(bf16[64,4,8,512]{3,2,1,0:T(8,128)(2,1)S(1)} %bitcast.80), kind=kOutput, calls=%fused_computation.7 | convolution fusion | flops 1073741824 | bytes 4194304 | tf_op jit(solution)/shard_map/dot_general | solution.py:82
  27.3 3.6 %gather_fusion = bf16[64,4,8,512]{3,2,1,0:T(8,128)(2,1)} fusion(bf16[4,64,8,512]{3,2,1,0:T(8,128)(2,1)} %convolution_bitcast_fusion, s32[1024]{0:T(1024)S(1)} %pad_clamp_fusion.1), kind=kCustom, calls=%fused_computation | custom fusion | bytes 4194560 | tf_op jit(solution)/shard_map/gather | solution.py:87
  30.9 2.5 all-to-all-done
  33.4 14.6 %all-to-all-start.3 = ((bf16[64,4,8,512]{3,2,1,0:T(8,128)(2,1)}), bf16[64,4,8,512]{3,2,1,0:T(8,128)(2,1)S(1)}, u32[]{:S(2)}, u32[]{:S(2)}) async-start(bf16[64,4,8,512]{3,2,1,0:T(8,128)(2,1)} %gather_fusion), calls=%async_computation.3 | async-start | bytes 4194304 | tf_op jit(solution)/shard_map/all_to_all | solution.py:27
  48.1 0.7 all-gather.2.cloned.1.call-update
  50.1 2.0 multiply_reduce_fusion
  53.1 52.6 %psum.35 = f32[64,4,4]{0,2,1:T(4,128)S(1)} all-reduce(f32[64,4,4]{0,2,1:T(4,128)S(1)} %broadcast_multiply_fusion), channel_id=1, replica_groups=mesh['group_0'=8,'group_1'=2,'group_2'=4,'replica_0'=2,'replica_1'=2] {'..., use_global_device_ids=true, to_apply=%region_3.0 | all-reduce | flops 1024 | bytes 8192 | tf_op jit(solution)/shard_map/psum | solution.py:15
  105.7 6.5 %psum.36 = f32[64,4,4]{0,2,1:T(4,128)S(1)} all-reduce(f32[64,4,4]{0,2,1:T(4,128)S(1)} %psum.35), channel_id=1, replica_groups=mesh['group_0'=8,'group_1'=2,'group_2'=4,'replica_0'=2,'replica_1'=2] {'..., use_global_device_ids=true, to_apply=%region_4.0 | all-reduce | flops 1024 | bytes 8192 | tf_op jit(solution)/shard_map/psum | solution.py:15
  112.2 8.7 %psum.37 = f32[64,4,4]{0,2,1:T(4,128)S(1)} all-reduce(f32[64,4,4]{0,2,1:T(4,128)S(1)} %psum.36), channel_id=1, replica_groups=mesh['group_0'=8,'group_1'=2,'group_2'=4,'replica_0'=2,'replica_1'=2] {'..., use_global_device_ids=true, to_apply=%region_5.0 | all-reduce | flops 1024 | bytes 8192 | tf_op jit(solution)/shard_map/psum | solution.py:15
  121.0 5.0 %psum.38 = f32[64,4,4]{0,2,1:T(4,128)S(1)} all-reduce(f32[64,4,4]{0,2,1:T(4,128)S(1)} %psum.37), channel_id=1, replica_groups=mesh['group_0'=8,'group_1'=2,'group_2'=4,'replica_0'=2,'replica_1'=2] {'..., use_global_device_ids=true, to_apply=%region_6.0 | all-reduce | flops 1024 | bytes 8192 | tf_op jit(solution)/shard_map/psum | solution.py:15
  126.0 2.5 psum.39
  131.8 0.8 broadcast_in_dim.98
  132.6 3.5 %all-to-all-start.2 = ((bf16[4,128,512]{2,1,0:T(8,128)(2,1)}), bf16[4,128,512]{2,1,0:T(8,128)(2,1)S(1)}, u32[]{:S(2)}, u32[]{:S(2)}) async-start(bf16[4,128,512]{2,1,0:T(8,128)(2,1)} %broadcast_in_dim.98), calls=%async_computation.2 | async-start | bytes 1048576 | tf_op jit(solution)/shard_map/all_to_all | solution.py:33
  136.4 34.0 %all-gather.2.cloned.1.call-done = bf16[4,512,512]{2,1,0:T(8,128)(2,1)} async-done(((bf16[4,8,512]{2,1,0:T(8,128)(2,1)}), bf16[4,512,512]{2,1,0:T(8,128)(2,1)}) %all-gather.2.cloned.1.call-update) | async-done | bytes 2097168 | tf_op jit(solution)/shard_map/all_gather | solution.py:91
  170.5 2.7 %fusion.29 = f32[4,8,512]{2,1,0:T(8,128)S(1)} fusion(bf16[4,512,512]{2,1,0:T(8,128)(2,1)} %all-gather.2.cloned.1.call-done, f32[4,8,512]{2,1,0:T(8,128)S(1)} %convert_reduce_fusion, f32[4]{0:T(128)S(1)} %multiply_add_fusion), kind=kOutput, calls=%fused_computation.31 | convolution fusion | flops 100679680 | bytes 2228240 | tf_op jit(solution)/shard_map/dot_general | solution.py:57
  173.2 0.9 fusion.53
  174.1 0.9 fusion.54
  175.0 0.9 fusion.55
  176.0 0.9 fusion.25
  176.9 1.6 stack.2
  178.5 7.8 %all-to-all-start.4 = ((bf16[64,4,8,512]{3,2,1,0:T(8,128)(2,1)}), bf16[64,4,8,512]{3,2,1,0:T(8,128)(2,1)S(1)}, u32[]{:S(2)}, u32[]{:S(2)}) async-start(bf16[64,4,8,512]{3,2,1,0:T(8,128)(2,1)} %stack.2), calls=%async_computation.4 | async-start | bytes 4194304 | tf_op jit(solution)/shard_map/all_to_all | solution.py:100
  186.6 46.7 %all-to-all-done.4 = bf16[64,4,8,512]{3,2,1,0:T(8,128)(2,1)S(1)} async-done(((bf16[64,4,8,512]{3,2,1,0:T(8,128)(2,1)}), bf16[64,4,8,512]{3,2,1,0:T(8,128)(2,1)S(1)}, u32[]{:S(2)}, u32[]{:S(2)}) %all-to-all-start.4) | async-done | bytes 2097184 | tf_op jit(solution)/shard_map/all_to_all | solution.py:100
  233.2 1.5 copy.61
  234.8 3.8 %gather_fusion.1 = bf16[64,4,8,512]{3,2,1,0:T(8,128)(2,1)} fusion(bf16[4,64,8,512]{3,2,1,0:T(8,128)(2,1)} %bitcast.79, s32[1024]{0:T(1024)S(1)} %pad_clamp_fusion), kind=kCustom, calls=%fused_computation.1 | custom fusion | bytes 4194560 | tf_op jit(solution)/shard_map/gather | solution.py:104
  238.5 5.4 %fusion.9 = bf16[512,4,512]{0,2,1:T(8,128)(2,1)} fusion(bf16[512,512,1]{1,0,2:T(8,128)(2,1)S(1)} %bitcast.84, f32[4]{0:T(128)S(1)} %get-tuple-element.20, bf16[64,4,8,512]{3,2,1,0:T(8,128)(2,1)S(1)} %bitcast.81, bf16[64,4,8,512]{3,2,1,0:T(8,128)(2,1)} %gather_fusion.1), kind=kOutput, calls=%fused_computation.16 | convolution fusion | flops 2152726528 | bytes 6815760 | tf_op jit(solution)/shard_map/dot_general | solution.py:112
  244.0 3.9 %copy.38 = bf16[512,2048]{1,0:T(8,128)(2,1)} copy(bf16[512,2048]{0,1:T(8,128)(2,1)} %bitcast.82) | data formatting | bytes 4194304
  (41 shorter events, 4.1 us)
Async XLA Ops:
  8.9 12.3 %all-to-all-start.1 = ((bf16[4,128,512]{2,1,0:T(8,128)(2,1)}), bf16[4,128,512]{2,1,0:T(8,128)(2,1)S(1)}, u32[]{:S(2)}, u32[]{:S(2)}) async-start(bf16[4,128,512]{2,1,0:T(8,128)(2,1)} %broadcast_in_dim.97), calls=%async_computation.1 | async-start | bytes 1048576 | tf_op jit(solution)/shard_map/all_to_all | solution.py:33
  13.0 11.6 %copy-start.1 = (bf16[512,2048]{1,0:T(8,128)(2,1)S(1)}, bf16[512,2048]{1,0:T(8,128)(2,1)}, u32[]{:S(2)}) copy-start(bf16[512,2048]{1,0:T(8,128)(2,1)} %param.6) | copy-start | bytes 6291460
  21.2 12.3 %all-to-all-start = ((bf16[4,128,512]{2,1,0:T(8,128)(2,1)}), bf16[4,128,512]{2,1,0:T(8,128)(2,1)S(1)}, u32[]{:S(2)}, u32[]{:S(2)}) async-start(bf16[4,128,512]{2,1,0:T(8,128)(2,1)} %bitcast.83), calls=%async_computation | async-start | bytes 1048576 | tf_op jit(solution)/shard_map/all_to_all | solution.py:27
  30.9 17.9 %copy-start.7 = (s32[64]{0:T(128)S(1)}, s32[64]{0:T(128)}, u32[]{:S(2)}) copy-start(s32[64]{0:T(128)} %param.11) | copy-start | bytes 772
  33.4 98.4 %all-to-all-start.3 = ((bf16[64,4,8,512]{3,2,1,0:T(8,128)(2,1)}), bf16[64,4,8,512]{3,2,1,0:T(8,128)(2,1)S(1)}, u32[]{:S(2)}, u32[]{:S(2)}) async-start(bf16[64,4,8,512]{3,2,1,0:T(8,128)(2,1)} %gather_fusion), calls=%async_computation.3 | async-start | bytes 4194304 | tf_op jit(solution)/shard_map/all_to_all | solution.py:27
  48.1 81.6 %copy-start.6 = (s32[4]{0:T(128)S(1)}, s32[4]{0:T(128)}, u32[]{:S(2)}) copy-start(s32[4]{0:T(128)} %param.10) | copy-start | bytes 52
  48.1 122.4 %all-gather.2.cloned.1.call-start = ((), (), s32[]{:S(2)}) async-start(), calls=%async_computation.5 | async-start | bytes 2129920 | tf_op jit(solution)/shard_map/all_gather | solution.py:91
  129.8 1.6 copy-start.3
  131.8 41.4 %copy-start.4 = (bf16[128,512]{1,0:T(8,128)(2,1)}, bf16[128,512]{1,0:T(8,128)(2,1)S(1)}, u32[]{:S(2)}) copy-start(bf16[128,512]{1,0:T(8,128)(2,1)S(1)} %fusion.23) | copy-start | bytes 393220
  132.6 44.3 %all-to-all-start.2 = ((bf16[4,128,512]{2,1,0:T(8,128)(2,1)}), bf16[4,128,512]{2,1,0:T(8,128)(2,1)S(1)}, u32[]{:S(2)}, u32[]{:S(2)}) async-start(bf16[4,128,512]{2,1,0:T(8,128)(2,1)} %broadcast_in_dim.98), calls=%async_computation.2 | async-start | bytes 1048576 | tf_op jit(solution)/shard_map/all_to_all | solution.py:33
  170.5 2.7 %copy-start = (bf16[4,512,512]{2,1,0:T(8,128)(2,1)S(1)}, bf16[4,512,512]{2,1,0:T(8,128)(2,1)}, u32[]{:S(2)}) copy-start(bf16[4,512,512]{2,1,0:T(8,128)(2,1)} %all-gather.2.cloned.1.call-done) | copy-start | bytes 6291460
  176.9 1.6 copy-start.5
  178.5 54.7 %all-to-all-start.4 = ((bf16[64,4,8,512]{3,2,1,0:T(8,128)(2,1)}), bf16[64,4,8,512]{3,2,1,0:T(8,128)(2,1)S(1)}, u32[]{:S(2)}, u32[]{:S(2)}) async-start(bf16[64,4,8,512]{3,2,1,0:T(8,128)(2,1)} %stack.2), calls=%async_computation.4 | async-start | bytes 4194304 | tf_op jit(solution)/shard_map/all_to_all | solution.py:100
  234.8 3.8 %copy-start.2 = (bf16[512,2048]{1,0:T(8,128)(2,1)S(1)}, bf16[512,2048]{1,0:T(8,128)(2,1)}, u32[]{:S(2)}) copy-start(bf16[512,2048]{1,0:T(8,128)(2,1)} %param.6) | copy-start | bytes 6291460
Sparse Core Ops, SparseCore 0:
  52.4 118.0 all-gather.1
